TPU v7x, 32 devices: a whole 2x2x4 slice. The times are simulated.
32 devices in a mesh: cell: 16 (over z, y, core), band: 2 (over x).
Axes of the slice: x: 2, y: 2, z: 4, core: 2. Of those that a mesh axis runs over, the one named last changes fastest.
Arguments:
- positions: bfloat16 [32, 3, 96, 192], P('cell', None, 'band'), may hold values from -6 to 6
- densities: bfloat16 [32, 3, 96, 192], P('cell', None, 'band'), may hold values from -6 to 6
- operator: bfloat16 [640, 96, 192], P('cell', 'band'), may hold values from -0.046875 to 0.046875
- target_shift: int32 [32, 16], P('cell'), may hold values from 0 to 191
- weights: float32 [640], replicated, may hold values from 0.02 to 0.2
Outputs:
- velocity: float32 [32, 3, 16], P('cell')
All inputs are finite; a program needn't handle non-finite values.
Results may differ from a plain program's by a relative error of at most 0.0003.
Values may be sent and summed in bfloat16 or wider, within the bound.
A program may use at most 64 MiB of HBM per device.

v0:
```python
import jax
import jax.numpy as jnp
from jax import lax
from jax.sharding import PartitionSpec as P

blob_radius = 0.5


def stokes(target, rows, weights):
    spread = target[:, :, :, None] - rows[:, 0:3]
    force = rows[:, 3:6]
    dist_sq = jnp.sum(spread * spread, axis=1)
    along = jnp.sum(spread * force, axis=1)
    blob_sq = blob_radius * blob_radius
    numer = (dist_sq + 2.0 * blob_sq)[:, None] * force + along[:, None] * spread
    kernel = weights / (dist_sq + blob_sq) ** 1.5
    return jnp.sum(numer * kernel[:, None], axis=-1)


def shifted_rows(source, shifts):
    caps_count, comps, lat_count, lon_count = source.shape
    doubled = jnp.concatenate([source, source], axis=3)
    zero = jnp.int32(0)

    def per_capsule(block, capsule_shifts):

        def per_target(offset):
            return lax.dynamic_slice(block, (zero, zero, offset), (comps, lat_count, lon_count))

        return jax.vmap(per_target)(capsule_shifts)

    rolled = jax.vmap(per_capsule)(doubled, shifts)
    rolled = jnp.transpose(rolled, (0, 2, 1, 3, 4))
    return rolled.reshape(caps_count * comps * shifts.shape[1], lat_count * lon_count)


def contract(left, right):
    return lax.dot_general(
        left, right, (((1,), (1,)), ((), ())), preferred_element_type=jnp.float32
    )


def per_device(positions, densities, operator, target_shift, weights):
    source = jnp.concatenate([positions, densities], axis=1)
    caps_here = source.shape[0]
    targets = target_shift.shape[1]
    rows = shifted_rows(source, target_shift)
    piece = lax.all_gather(operator, "cell", axis=0, tiled=True)
    rotated = contract(rows, piece.reshape(piece.shape[0], -1))
    partial_value = rotated.reshape(caps_here, 6, targets, -1)
    summed = lax.psum(partial_value, "band")
    velocity = stokes(summed[:, 0:3, :, 0], summed, weights)
    return velocity


def solution(mesh):
    in_specs = (
        P("cell", None, "band", None),
        P("cell", None, "band", None),
        P("cell", "band", None),
        P("cell", None),
        P(),
    )
    out_specs = P("cell", None, None)
    return jax.shard_map(
        per_device, mesh=mesh, in_specs=in_specs, out_specs=out_specs, check_vma=False
    )
```

profile of v0, /device:TPU:0, one launch (start us, length us, event | category | flops | bytes accessed | tf_op | source)
XLA Modules:
  0.0 182.1 jit_solution(361846499358096142)
XLA Ops:
  6.5 0.0 copy-start.1
  6.5 0.0 all-gather.2.cloned.1.call-start
  6.5 2.5 %copy.14 = bf16[40,48,192]{2,0,1:T(8,128)(2,1)} copy(bf16[40,48,192]{2,1,0:T(8,128)(2,1)} %param.7) | data formatting | bytes 1474560 | tf_op args[2]
  9.1 0.0 all-gather.2.cloned.1.call-update
  9.1 0.0 all-reduce.3.cloned.1.call-start
  9.1 1.3 maximum_maximum_fusion
  10.4 1.2 copy.12
  11.7 0.0 copy-done.1
  11.7 0.1 reshape.15
  11.8 8.6 %gather_fusion = bf16[32,6,48,192]{2,1,3,0:T(8,128)(2,1)} fusion(bf16[2,6,48,384]{2,1,0,3:T(8,128)(2,1)S(1)} %copy.12, s32[32]{0:T(128)S(1)} %reshape.15), kind=kCustom, calls=%fused_computation | custom fusion | bytes 7078400 | tf_op jit(solution)/shard_map/vmap(vmap())/gather | solution.py:28
  20.4 14.0 %copy.13 = bf16[2,16,6,48,192]{4,1,3,2,0:T(8,128)(2,1)} copy(bf16[2,16,6,48,192]{3,2,4,1,0:T(8,128)(2,1)} %bitcast.23) | data formatting | bytes 7077888 | tf_op jit(solution)/shard_map/vmap(vmap())/gather | solution.py:28
  34.4 0.0 copy-start
  34.4 97.8 %all-gather.2.cloned.1.call-done = bf16[640,48,192]{2,0,1:T(8,128)(2,1)} async-done(((bf16[40,48,192]{2,0,1:T(8,128)(2,1)}), bf16[640,48,192]{2,0,1:T(8,128)(2,1)}) %all-gather.2.cloned.1.call-update) | async-done | bytes 11796496 | tf_op jit(solution)/shard_map/all_gather | solution.py:48
  132.2 12.8 %fusion.3 = f32[2,6,16,640]{3,2,1,0:T(8,128)} fusion(bf16[640,48,192]{2,0,1:T(8,128)(2,1)} %all-gather.2.cloned.1.call-done, bf16[2,16,6,48,192]{4,1,3,2,0:T(8,128)(2,1)} %copy.13), kind=kOutput, calls=%fused_computation.4 | convolution fusion | flops 2264924160 | bytes 15826944 | tf_op jit(solution)/shard_map/dot_general | solution.py:38
  145.0 0.0 all-reduce.3.cloned.1.call-update
  145.0 26.2 %all-reduce.3.cloned.1.call-done = f32[2,6,16,640]{3,2,1,0:T(8,128)} async-done(((f32[2,6,16,640]{3,2,1,0:T(8,128)}), f32[2,6,16,640]{3,2,1,0:T(8,128)}) %all-reduce.3.cloned.1.call-update) | async-done | bytes 491536 | tf_op jit(solution)/shard_map/psum | solution.py:51
  171.2 0.8 slice.19
  172.0 0.1 copy.15
  172.1 1.2 multiply_reduce_fusion.1
  173.3 0.0 copy-done
  173.4 1.3 multiply_reduce_fusion
  174.7 0.6 copy.17
  (3 shorter events, 0.1 us)
Async XLA Ops:
  6.5 5.1 %copy-start.1 = (s32[2,16]{1,0:T(2,128)S(1)}, s32[2,16]{1,0:T(2,128)}, u32[]{:S(2)}) copy-start(s32[2,16]{1,0:T(2,128)} %param.8) | copy-start | bytes 388
  6.5 125.7 %all-gather.2.cloned.1.call-start = ((), (), s32[]{:S(2)}) async-start(), calls=%async_computation | async-start | bytes 16711680 | tf_op jit(solution)/shard_map/all_gather | solution.py:48
  9.1 162.2 %all-reduce.3.cloned.1.call-start = ((), (), s32[]{:S(2)}) async-start(), calls=%async_computation.1 | async-start | bytes 983040 | tf_op jit(solution)/shard_map/psum | solution.py:51
  34.4 139.0 %copy-start = (f32[640]{0:T(1024)S(1)}, f32[640]{0:T(1024)}, u32[]{:S(2)}) copy-start(f32[640]{0:T(1024)} %param.9) | copy-start | bytes 7684
Sparse Core Ops, SparseCore 0:
  9.7 122.4 all-gather.1
  145.2 26.0 all-reduce.2
where the time goes:
time: 182 us
  waiting for transfers between devices  124 us (68%)
  local copies, waits for them, and re-layouts  27.9 us (15%)
  between operations  13.5 us (7%)
  matrix products  12.8 us (7%)
  other arithmetic  3.8 us (2%)
    all_gather x1, waiting for transfers between devices, per_device(): piece = lax.all_gather(operator, 'cell', axis=0, tiled=True)  97.8 us
    psum x1, waiting for transfers between devices, per_device(): summed = lax.psum(partial_value, 'band')  26.2 us
    gather x3, local copies, waits for them, and re-layouts, per_target(): lax.dynamic_slice(block, (zero, zero, offset), (comps, lat_count, lon_cou...  22.7 us
    dot_general x1, matrix products, contract(): lax.dot_general(left, right, (((1,), (1,)), ((), ())), preferred_element_...  12.8 us
  transfers between devices with their start and end apart: 2, of which 2 were waited for; matrix products, arithmetic and copies ran while one was open for 14% of the time, Pallas kernels for 0%

commit v1 on v0

v1 whole, which is shorter than its diff:
```python
import functools

import jax
import jax.numpy as jnp
from jax import lax
from jax.experimental import pallas as pl
from jax.experimental.pallas import tpu as pltpu
from jax.sharding import PartitionSpec as P

blob_radius = 0.5
MESH = pl.DeviceIdType.MESH
LANES = 128
GROUP = 8


def kernel(dims, src_ref, shift_ref, op_ref, weight_ref, out_ref, srcbuf, shiftbuf, opbuf,
           rolled, acc, xbuf, x0buf, vbuf, fin, src_send, src_recv, shift_send, shift_recv,
           op_send, op_recv, own_sem, x_send, x_recv, x0_send, x0_recv, fin_send, fin_recv):
    nz, nq, nb, caps, targets, pairs, rows, rows_pad, lon, chunks = dims
    cell, band = lax.axis_index("cell"), lax.axis_index("band")
    z, q = cell // nq, cell % nq
    depth = opbuf.shape[2]
    step = depth // chunks
    span = targets * GROUP
    keep = nz * caps // nb
    src_rows = pairs * GROUP
    side = q + 1 - 2 * (q % 2)
    across = (q + 2) % nq

    def cell_of(zz, qq):
        return zz * nq + qq

    barrier = pltpu.get_barrier_semaphore()
    for dz in range(nz):
        for db in range(nb):
            if dz or db:
                pl.semaphore_signal(barrier, inc=1, device_id=(cell_of((z + dz) % nz, q), (band + db) % nb), device_id_type=MESH)
    pl.semaphore_signal(barrier, inc=1, device_id=(cell_of(z, side), band), device_id_type=MESH)
    pl.semaphore_signal(barrier, inc=1, device_id=(cell_of(z, across), band), device_id_type=MESH)
    own = [pltpu.make_async_copy(src_ref, srcbuf.at[z], own_sem.at[0]),
           pltpu.make_async_copy(shift_ref, shiftbuf.at[z], own_sem.at[1]),
           pltpu.make_async_copy(op_ref, opbuf.at[q], own_sem.at[2])]
    for copy in own:
        copy.start()
    pl.semaphore_wait(barrier, nz * nb - 1 + 2)

    def op_copy(source, slot, part, target, lane):
        return pltpu.make_async_remote_copy(
            src_ref=source, dst_ref=opbuf.at[slot, :, pl.ds(part * step, step)],
            send_sem=op_send.at[lane, part], recv_sem=op_recv.at[lane, part],
            device_id=(cell_of(z, target), band), device_id_type=MESH)

    def src_copy(origin, dz):
        return pltpu.make_async_remote_copy(
            src_ref=src_ref, dst_ref=srcbuf.at[origin], send_sem=src_send.at[dz], recv_sem=src_recv.at[dz],
            device_id=(cell_of((z + dz) % nz, q), band), device_id_type=MESH)

    def shift_copy(origin, dz):
        return pltpu.make_async_remote_copy(
            src_ref=shift_ref, dst_ref=shiftbuf.at[origin], send_sem=shift_send.at[dz], recv_sem=shift_recv.at[dz],
            device_id=(cell_of((z + dz) % nz, q), band), device_id_type=MESH)

    to_across = [op_copy(op_ref.at[:, pl.ds(p * step, step)], q, p, across, 0) for p in range(chunks)]
    to_side = [op_copy(op_ref.at[:, pl.ds(p * step, step)], q, p, side, 1) for p in range(chunks)]
    forward = [op_copy(opbuf.at[across, :, pl.ds(p * step, step)], across, p, side, 2) for p in range(chunks)]
    order = [dz for d in range(1, nz // 2 + 1) for dz in ((d, nz - d) if d != nz - d else (d,))]
    for copy in to_across:
        copy.start()
    for dz in order:
        shift_copy(z, dz).start()
        src_copy(z, dz).start()
    for copy in to_side:
        copy.start()

    def roll(zz):
        lane_code = lax.broadcasted_iota(jnp.int32, (3 * LANES, 2 * LANES), 0)
        low = lon - LANES
        lane_code = jnp.where(lane_code < lon, lane_code,
                              jnp.where(lane_code < 2 * LANES, lane_code + 2 * low, lane_code - low))
        lane = lax.broadcasted_iota(jnp.int32, (1, LANES), 1)

        def wrap(value):
            return jnp.where(value >= lon, value - lon, value)

        def body(index, carry):
            cap, pair = index // (targets // 2), index % (targets // 2)
            goal = [[], [], []]
            for side_t in range(2):
                shift = shiftbuf[zz, pl.ds(cap * targets + pair * 2 + side_t, 1), :]
                first = wrap(lane + shift)
                goal[0].append(first)
                goal[1].append(first + lon)
                goal[2].append(jnp.where(lane < low, wrap(wrap(lane + LANES + shift - 0)), wrap(wrap(lane + LANES - low + shift)) + lon))
            base = pl.multiple_of(cap * src_rows, src_rows)
            for tile in range(3):
                wanted = jnp.concatenate(goal[tile], axis=1)
                begin, end = ((0, 2), (1, 3), (0, 3))[tile]
                hit = lane_code[begin * LANES:end * LANES] == wanted
                pick = jnp.where(hit, 1.0, 0.0).astype(jnp.bfloat16)
                moved = jnp.dot(srcbuf[zz, pl.ds(base, src_rows), begin * LANES:end * LANES], pick,
                                preferred_element_type=jnp.float32)
                row = pl.multiple_of((cap * nz + zz) * span + pair * 2 * GROUP, 2 * GROUP)
                for p in range(pairs):
                    both = jnp.concatenate([moved[p * GROUP:(p + 1) * GROUP, :LANES],
                                            moved[p * GROUP:(p + 1) * GROUP, LANES:]], axis=0)
                    rolled[pl.ds(row, 2 * GROUP), pl.ds((p * 3 + tile) * LANES, LANES)] = both.astype(jnp.bfloat16)
            return carry

        lax.fori_loop(0, caps * targets // 2, body, 0)

    own[0].wait()
    own[1].wait()
    roll(z)
    sent = 0
    for dz in order:
        zz = (z + nz - dz) % nz
        shift_copy(zz, dz).wait_recv()
        src_copy(zz, dz).wait_recv()
        roll(zz)
        if sent < chunks - 1:
            to_across[sent].wait_recv()
            forward[sent].start()
            sent += 1
    while sent < chunks:
        to_across[sent].wait_recv()
        forward[sent].start()
        sent += 1
    own[2].wait()
    for copy in to_side:
        copy.wait_recv()

    for p in range(chunks):
        forward[p].wait_recv()
        blocks = opbuf[:, :, pl.ds(p * step, step)].reshape(nq * rows_pad, step)

        def multiply(index, carry):
            at = pl.multiple_of(index * 2 * span, 2 * span)
            part = lax.dot_general(blocks, rolled[pl.ds(at, 2 * span), pl.ds(p * step, step)],
                                   (((1,), (1,)), ((), ())), preferred_element_type=jnp.float32)
            for half in range(2):
                where = index * 2 + half
                piece = part[:, half * span:(half + 1) * span]
                if p == 0:
                    acc[where] = piece
                else:
                    acc[where] += piece
            return carry

        lax.fori_loop(0, nz * caps // 2, multiply, 0)

    def x_copy(db, block, origin):
        target = (band + db) % nb
        return pltpu.make_async_remote_copy(
            src_ref=acc.at[pl.ds(target * keep, keep), pl.ds(block * rows_pad, rows_send), :],
            dst_ref=xbuf.at[origin, :, pl.ds(block * rows_pad, rows_send), :],
            send_sem=x_send.at[db, block], recv_sem=x_recv.at[db, block],
            device_id=(cell, target), device_id_type=MESH)

    rows_send = (rows + GROUP - 1) // GROUP * GROUP
    for db in range(1, nb):
        for block in range(nq):
            x_copy(db, block, band).start()
    for db in range(1, nb):
        for block in range(nq):
            x_copy(db, block, (band + nb - db) % nb).wait_recv()

    def total(i, block):
        value = acc[band * keep + i, block * rows_pad:block * rows_pad + rows_send, :]
        for db in range(1, nb):
            value = value + xbuf[(band + nb - db) % nb, i, block * rows_pad:block * rows_pad + rows_send, :]
        return value

    def x0_copy(dz):
        return pltpu.make_async_remote_copy(
            src_ref=x0buf, dst_ref=x0buf, send_sem=x0_send.at[dz], recv_sem=x0_recv.at[0],
            device_id=(cell_of(dz, q), band), device_id_type=MESH)

    @pl.when(z == 0)
    def _():
        for i in range(keep):
            x0buf[i] = total(i, 0)[0:GROUP]
        for dz in range(1, nz):
            x0_copy(dz).start()

    @pl.when(z != 0)
    def _():
        x0_copy(1).wait_recv()

    lane = lax.broadcasted_iota(jnp.int32, (1, span), 1) % GROUP
    blob_sq = blob_radius * blob_radius

    def fin_copy(i, x, origin_cap, origin_z):
        return pltpu.make_async_remote_copy(
            src_ref=vbuf.at[i], dst_ref=fin.at[origin_cap, origin_z], send_sem=fin_send.at[i, x],
            recv_sem=fin_recv.at[origin_cap, origin_z],
            device_id=(cell_of((band * keep + i) % nz, q), x), device_id_type=MESH)

    def three(value):
        value = jnp.where(lane < 3, value, 0.0)
        value = value + pltpu.roll(value, 1, 1) + pltpu.roll(value, 2, 1)
        value = jnp.where(lane == 2, value, 0.0)
        return value + pltpu.roll(value, span - 1, 1) + pltpu.roll(value, span - 2, 1)

    for i in range(keep):
        velocity = jnp.zeros((GROUP, span), jnp.float32)
        for block in range(nq):
            value = total(i, block)
            spread = x0buf[i, 0:1] - value
            force = pltpu.roll(value, span - 3, 1)
            dist_sq = three(spread * spread)
            along = three(spread * force)
            inverse = lax.rsqrt(dist_sq + blob_sq)
            share = weight_ref[block * rows_pad:block * rows_pad + rows_send, :] * (inverse * inverse * inverse)
            term = ((dist_sq + 2.0 * blob_sq) * force + along * spread) * share
            term = jnp.where(lane < 3, term, 0.0)
            for k in range(rows_send // GROUP):
                velocity = velocity + term[k * GROUP:(k + 1) * GROUP]
        vbuf[i] = velocity
        g = band * keep + i
        for x in range(nb):
            itself = jnp.logical_and(g % nz == z, band == x)

            @pl.when(itself)
            def _():
                fin[g // nz, z] = velocity

            @pl.when(jnp.logical_not(itself))
            def _():
                fin_copy(i, x, g // nz, z).start()

    for cap in range(caps):
        for zz in range(nz):
            itself = jnp.logical_and(z == zz, (cap * nz + z) // keep == band)

            @pl.when(jnp.logical_not(itself))
            def _():
                fin_copy(0, 0, cap, zz).wait_recv()

    out_ref[...] = jnp.zeros_like(out_ref)
    for cap in range(caps):
        value = fin[cap, 0]
        for zz in range(1, nz):
            value = value + fin[cap, zz]
        out_ref[cap:cap + 1, :] = jnp.sum(value, axis=0, keepdims=True)

    for copy in to_across + to_side + forward:
        copy.wait_send()
    for dz in order:
        shift_copy(z, dz).wait_send()
        src_copy(z, dz).wait_send()
    for db in range(1, nb):
        for block in range(nq):
            x_copy(db, block, band).wait_send()

    @pl.when(z == 0)
    def _():
        for dz in range(1, nz):
            x0_copy(dz).wait_send()

    for i in range(keep):
        for x in range(nb):
            itself = jnp.logical_and((band * keep + i) % nz == z, band == x)

            @pl.when(jnp.logical_not(itself))
            def _():
                fin_copy(i, x, 0, 0).wait_send()


def per_device(cells, bands, positions, densities, operator, target_shift, weights):
    caps, comps, lat, lon = positions.shape
    targets = target_shift.shape[1]
    rows = operator.shape[0]
    nq = 4
    nz = cells // nq
    pairs = lat // 2
    rows_pad = (rows + 15) // 16 * 16
    rows_send = (rows + 7) // 8 * 8
    depth = lat * lon
    chunks = 4 if (depth // LANES) % 4 == 0 else 2
    span = targets * GROUP
    keep = nz * caps // bands

    def tiles(array):
        lead = array.shape[:-2]
        high = array[..., :LANES].reshape(lead + (pairs, 2, LANES))
        low = array[..., LANES:].reshape(lead + (pairs, LANES))
        return high[..., 0, :], high[..., 1, :], low

    first, second, low = tiles(operator)
    op = jnp.stack([first, second, low], axis=2).reshape(rows, depth)
    op = jnp.pad(op, ((0, rows_pad - rows), (0, 0)))
    source = jnp.concatenate([positions, densities], axis=1)
    source = jnp.pad(source, ((0, 0), (0, GROUP - 2 * comps), (0, 0), (0, 0)))
    source = jnp.transpose(source.reshape(caps, GROUP, pairs, 2, lon), (0, 2, 1, 3, 4))
    first, second = source[..., 0, :], source[..., 1, :]
    source = jnp.concatenate([first, second[..., LANES:], second[..., :LANES]], axis=-1)
    source = source.reshape(caps * pairs * GROUP, 3 * LANES)
    shifts = jnp.broadcast_to(target_shift.reshape(caps * targets, 1), (caps * targets, LANES))
    z = lax.axis_index("cell") // nq
    mine = lax.dynamic_slice(weights, (z * nq * rows,), (nq * rows,)).reshape(nq, rows)
    mine = jnp.pad(mine, ((0, 0), (0, rows_pad - rows))).reshape(nq * rows_pad, 1)
    mine = jnp.broadcast_to(mine, (nq * rows_pad, span))
    dims = (nz, nq, bands, caps, targets, pairs, rows, rows_pad, lon, chunks)
    dma = pltpu.SemaphoreType.DMA
    hbm = pl.BlockSpec(memory_space=pl.ANY)
    vmem = pl.BlockSpec(memory_space=pltpu.VMEM)
    out = pl.pallas_call(
        functools.partial(kernel, dims),
        out_shape=jax.ShapeDtypeStruct((GROUP, span), jnp.float32),
        in_specs=[hbm, hbm, hbm, vmem],
        out_specs=vmem,
        scratch_shapes=[
            pltpu.VMEM((nz,) + source.shape, jnp.bfloat16),
            pltpu.VMEM((nz, caps * targets, LANES), jnp.int32),
            pltpu.VMEM((nq, rows_pad, depth), jnp.bfloat16),
            pltpu.VMEM((nz * caps * span, depth), jnp.bfloat16),
            pltpu.VMEM((nz * caps, nq * rows_pad, span), jnp.float32),
            pltpu.VMEM((bands, keep, nq * rows_pad, span), jnp.float32),
            pltpu.VMEM((keep, GROUP, span), jnp.float32),
            pltpu.VMEM((keep, GROUP, span), jnp.float32),
            pltpu.VMEM((caps, nz, GROUP, span), jnp.float32),
            dma((nz,)), dma((nz,)), dma((nz,)), dma((nz,)),
            dma((3, chunks)), dma((3, chunks)), dma((3,)),
            dma((bands, nq)), dma((bands, nq)), dma((nz,)), dma((1,)),
            dma((keep, bands)), dma((caps, nz)),
        ],
        compiler_params=pltpu.CompilerParams(
            collective_id=0, has_side_effects=True, vmem_limit_bytes=60 * 1024 * 1024
        ),
    )(source, shifts, op, mine)
    velocity = out[:caps].reshape(caps, targets, GROUP)[:, :, :comps]
    return jnp.transpose(velocity, (0, 2, 1))


def solution(mesh):
    in_specs = (
        P("cell", None, "band", None),
        P("cell", None, "band", None),
        P("cell", "band", None),
        P("cell", None),
        P(),
    )
    out_specs = P("cell", None, None)
    body = functools.partial(per_device, mesh.shape["cell"], mesh.shape["band"])
    return jax.shard_map(body, mesh=mesh, in_specs=in_specs, out_specs=out_specs, check_vma=False)
```

time: 182 us -> 77.3 us (0.42)
  waiting for transfers between devices: 124 us -> 0 us
  Pallas kernels: 0 us -> 67.2 us
  local copies, waits for them, and re-layouts: 27.9 us -> 6.89 us
  between operations: 13.5 us -> 0.09 us
  matrix products: 12.8 us -> 0 us
    all_gather x1 -> x0, waiting for transfers between devices: 97.8 us -> none  [per_device(): piece = lax.all_gather(operator, 'cell', axis=0, tiled=True)]
    pallas_call x0 -> x1, Pallas kernels: none -> 67.2 us  [per_device(): pl.pallas_call(functools.partial(kernel, dims), out_shape=jax.ShapeDtypeS...]
    psum x1 -> x0, waiting for transfers between devices: 26.2 us -> none  [per_device(): summed = lax.psum(partial_value, 'band')]
    gather x3 -> x0, local copies, waits for them, and re-layouts: 22.7 us -> none  [per_target(): lax.dynamic_slice(block, (zero, zero, offset), (comps, lat_count, lon_cou...]
    dot_general x1 -> x0, matrix products: 12.8 us -> none  [contract(): lax.dot_general(left, right, (((1,), (1,)), ((), ())), preferred_element_...]
    unnamed x5 -> x2, local copies, waits for them, and re-layouts: 2.53 us -> 0.01 us
    reduce_sum x2 -> x0, other arithmetic: 2.45 us -> none  [the longest x1 1.26 us: stokes(): return jnp.sum(numer * kernel[:, None], axis=-1)]
  transfers between devices with their start and end apart: 2 -> 0, of which waited for: 2 -> 0; matrix products, arithmetic and copies ran while one was open for 14% -> 0% of each run, Pallas kernels for 0% -> 0%
where the time goes in v1:
time: 77.3 us; the launch traced here: 77.1 us
  Pallas kernels  67.2 us (87%)
  local copies, waits for them, and re-layouts  6.89 us (9%)
  other arithmetic  2.89 us (4%)
    pallas_call x1, Pallas kernels, per_device(): pl.pallas_call(functools.partial(kernel, dims), out_shape=jax.ShapeDtypeS...  67.2 us

profile of v1, /device:TPU:0, one launch (start us, length us, event | category | flops | bytes accessed | tf_op | source)
XLA Modules:
  0.0 77.1 jit_solution(13550129214387889007)
XLA Ops:
  0.0 1.0 %fusion.2 = bf16[2,8,48,192]{3,2,1,0:T(8,128)(2,1)S(1)} fusion(bf16[2,3,48,192]{3,2,1,0:T(8,128)(2,1)} %param.6, bf16[2,3,48,192]{3,2,1,0:T(8,128)(2,1)} %param.5), kind=kLoop, calls=%fused_computation.4 | loop fusion | flops 1032192 | bytes 516096 | tf_op jit(solution)/shard_map/concatenate | solution.py:292
  1.0 0.2 reshape.24
  1.2 0.1 copy.13
  1.4 0.0 copy-start
  1.4 0.0 slice-start
  1.5 0.8 %pad_maximum_fusion.1.src_ref = bf16[384,384]{1,0:T(8,128)(2,1)} fusion(bf16[384,128]{1,0:T(8,128)(2,1)S(1)} %bitcast.16, bf16[384,64]{1,0:T(8,128)(2,1)S(1)} %bitcast.17, bf16[384,192]{1,0:T(8,128)(2,1)S(1)} %bitcast.15), kind=kLoop, calls=%fused_computation.6 | loop fusion | flops 884736 | bytes 589824 | tf_op jit(solution)/shard_map/concatenate | solution.py:296
  2.3 0.0 copy-done
  2.3 0.1 broadcast_in_dim.14
  2.4 0.7 broadcast_in_dim.15.shift_ref
  3.1 0.0 slice-done
  3.1 0.0 slice-start.1
  3.1 0.3 stack_reshape.4
  3.4 0.7 slice-done.1
  4.1 1.0 %pad_maximum_fusion = bf16[40,24,3,128]{3,2,1,0:T(4,128)(2,1)S(1)} fusion(bf16[40,24,1,128]{3,2,1,0:T(2,128)(2,1)S(1)} %stack_reshape.4, bf16[40,24,2,128]{3,2,1,0:T(2,128)(2,1)S(1)} %bitcast.13), kind=kLoop, calls=%fused_computation | loop fusion | flops 1474560 | bytes 1474560 | tf_op jit(solution)/shard_map/stack | solution.py:290
  5.1 0.7 reshape.26
  5.8 1.0 %pad.13.op_ref = bf16[48,9216]{1,0:T(8,128)(2,1)} pad(bf16[40,9216]{1,0:T(8,128)(2,1)S(1)} %reshape.26, bf16[]{:T(256)} %constant.21.clone.1), padding=0_8x0_0 | pad | bytes 1622018 | tf_op jit(solution)/shard_map/jit(_pad)/pad | solution.py:291
  6.8 0.8 dynamic_slice.3
  7.5 0.1 reshape.27
  7.6 0.1 broadcast_in_dim.16
  7.7 0.7 broadcast_in_dim.17.weight_ref
  8.4 67.2 %shard_map.55 = f32[8,128]{1,0:T(8,128)} custom-call(bf16[384,384]{1,0:T(8,128)(2,1)} %pad_maximum_fusion.1.src_ref, s32[32,128]{1,0:T(8,128)} %broadcast_in_dim.15.shift_ref, bf16[48,9216]{1,0:T(8,128)(2,1)} %pad.13.op_ref, f32[192,128]{1,0:T(8,128)} %broadcast_in_dim.17.weight_ref), custom_call_target="tpu_custom_call" | custom-call | tf_op jit(solution)/shard_map/pallas_call | solution.py:307
  75.6 0.7 slice.33
  76.3 0.1 reshape.28
  76.4 0.7 copy.11
  (5 shorter events, 0.1 us)
Async XLA Ops:
  1.4 0.9 %copy-start = (s32[2,16]{1,0:T(2,128)S(1)}, s32[2,16]{1,0:T(2,128)}, u32[]{:S(2)}) copy-start(s32[2,16]{1,0:T(2,128)} %param.8) | copy-start | bytes 388
  1.4 1.6 %slice-start = ((bf16[40,48,192]{2,1,0:T(8,128)(2,1)}), bf16[40,48,64]{2,1,0:T(8,128)(2,1)S(1)}, s32[]{:S(2)}) async-start(bf16[40,48,192]{2,1,0:T(8,128)(2,1)} %param.7), calls=%async_computation | async-start | bytes 983040 | tf_op jit(solution)/shard_map/slice | solution.py:286
  3.1 1.0 %slice-start.1 = ((bf16[40,48,192]{2,1,0:T(8,128)(2,1)}), bf16[40,48,128]{2,1,0:T(8,128)(2,1)S(1)}, s32[]{:S(2)}) async-start(bf16[40,48,192]{2,1,0:T(8,128)(2,1)} %param.7), calls=%async_computation.1 | async-start | bytes 983040 | tf_op jit(solution)/shard_map/slice | solution.py:285

commit v2 on v1

--- a/solution.py
+++ b/solution.py
@@ -13,7 +13,7 @@
 GROUP = 8
 
 
-def kernel(dims, src_ref, shift_ref, op_ref, weight_ref, out_ref, srcbuf, shiftbuf, opbuf,
+def kernel(dims, src_ref, shift_ref, op_ref, weight_ref, out_ref, srcbuf, shiftbuf, opbuf, wide,
            rolled, acc, xbuf, x0buf, vbuf, fin, src_send, src_recv, shift_send, shift_recv,
            op_send, op_recv, own_sem, x_send, x_recv, x0_send, x0_recv, fin_send, fin_recv):
     nz, nq, nb, caps, targets, pairs, rows, rows_pad, lon, chunks = dims
@@ -24,6 +24,7 @@
     span = targets * GROUP
     keep = nz * caps // nb
     src_rows = pairs * GROUP
+    comps = srcbuf.shape[2] // pairs
     side = q + 1 - 2 * (q % 2)
     across = (q + 2) % nq
 
@@ -50,25 +51,29 @@
             send_sem=op_send.at[lane, part], recv_sem=op_recv.at[lane, part],
             device_id=(cell_of(z, target), band), device_id_type=MESH)
 
-    def src_copy(origin, dz):
-        return pltpu.make_async_remote_copy(
-            src_ref=src_ref, dst_ref=srcbuf.at[origin], send_sem=src_send.at[dz], recv_sem=src_recv.at[dz],
-            device_id=(cell_of((z + dz) % nz, q), band), device_id_type=MESH)
-
-    def shift_copy(origin, dz):
-        return pltpu.make_async_remote_copy(
-            src_ref=shift_ref, dst_ref=shiftbuf.at[origin], send_sem=shift_send.at[dz], recv_sem=shift_recv.at[dz],
-            device_id=(cell_of((z + dz) % nz, q), band), device_id_type=MESH)
+    def line_copy(origin, way, first):
+        lane = 2 * way + (0 if first else 1)
+        target = (cell_of(z + 1 - 2 * way, q), band)
+        return (pltpu.make_async_remote_copy(
+            src_ref=shift_ref if first else shiftbuf.at[origin], dst_ref=shiftbuf.at[origin],
+            send_sem=shift_send.at[lane, origin], recv_sem=shift_recv.at[origin],
+            device_id=target, device_id_type=MESH), pltpu.make_async_remote_copy(
+            src_ref=src_ref if first else srcbuf.at[origin], dst_ref=srcbuf.at[origin],
+            send_sem=src_send.at[lane, origin], recv_sem=src_recv.at[origin],
+            device_id=target, device_id_type=MESH))
+
+    inner = (z < nz - 1, z > 0)
 
     to_across = [op_copy(op_ref.at[:, pl.ds(p * step, step)], q, p, across, 0) for p in range(chunks)]
     to_side = [op_copy(op_ref.at[:, pl.ds(p * step, step)], q, p, side, 1) for p in range(chunks)]
     forward = [op_copy(opbuf.at[across, :, pl.ds(p * step, step)], across, p, side, 2) for p in range(chunks)]
-    order = [dz for d in range(1, nz // 2 + 1) for dz in ((d, nz - d) if d != nz - d else (d,))]
     for copy in to_across:
         copy.start()
-    for dz in order:
-        shift_copy(z, dz).start()
-        src_copy(z, dz).start()
+    for way in range(2):
+        @pl.when(inner[way])
+        def _():
+            for copy in line_copy(z, way, True):
+                copy.start()
     for copy in to_side:
         copy.start()
 
@@ -81,6 +86,14 @@
 
         def wrap(value):
             return jnp.where(value >= lon, value - lon, value)
+
+        grid = (src_rows, pairs * comps)
+        at, of = lax.broadcasted_iota(jnp.int32, grid, 0), lax.broadcasted_iota(jnp.int32, grid, 1)
+        spread_out = jnp.logical_and(at % GROUP < comps, of == at // GROUP * comps + at % GROUP)
+        spread_out = jnp.where(spread_out, 1.0, 0.0).astype(jnp.bfloat16)
+        for cap in range(caps):
+            wide[cap * src_rows:(cap + 1) * src_rows, :] = jnp.dot(
+                spread_out, srcbuf[zz, cap], preferred_element_type=jnp.float32).astype(jnp.bfloat16)
 
         def body(index, carry):
             cap, pair = index // (targets // 2), index % (targets // 2)
@@ -97,7 +110,7 @@
                 begin, end = ((0, 2), (1, 3), (0, 3))[tile]
                 hit = lane_code[begin * LANES:end * LANES] == wanted
                 pick = jnp.where(hit, 1.0, 0.0).astype(jnp.bfloat16)
-                moved = jnp.dot(srcbuf[zz, pl.ds(base, src_rows), begin * LANES:end * LANES], pick,
+                moved = jnp.dot(wide[pl.ds(base, src_rows), begin * LANES:end * LANES], pick,
                                 preferred_element_type=jnp.float32)
                 row = pl.multiple_of((cap * nz + zz) * span + pair * 2 * GROUP, 2 * GROUP)
                 for p in range(pairs):
@@ -112,11 +125,28 @@
     own[1].wait()
     roll(z)
     sent = 0
-    for dz in order:
-        zz = (z + nz - dz) % nz
-        shift_copy(zz, dz).wait_recv()
-        src_copy(zz, dz).wait_recv()
-        roll(zz)
+    for d in range(1, nz):
+        for way in range(2):
+            origin = (z - d, z + d)[way]
+            there = (z >= d, z + d < nz)[way]
+
+            @pl.when(there)
+            def _():
+                for copy in line_copy(origin, way, False):
+                    copy.wait_recv()
+
+            @pl.when(jnp.logical_and(there, inner[way]))
+            def _():
+                for copy in line_copy(origin, way, False):
+                    copy.start()
+
+        for way in range(2):
+            origin = (z - d, z + d)[way]
+            there = (z >= d, z + d < nz)[way]
+
+            @pl.when(there)
+            def _():
+                roll(origin)
         if sent < chunks - 1:
             to_across[sent].wait_recv()
             forward[sent].start()
@@ -129,24 +159,7 @@
     for copy in to_side:
         copy.wait_recv()
 
-    for p in range(chunks):
-        forward[p].wait_recv()
-        blocks = opbuf[:, :, pl.ds(p * step, step)].reshape(nq * rows_pad, step)
-
-        def multiply(index, carry):
-            at = pl.multiple_of(index * 2 * span, 2 * span)
-            part = lax.dot_general(blocks, rolled[pl.ds(at, 2 * span), pl.ds(p * step, step)],
-                                   (((1,), (1,)), ((), ())), preferred_element_type=jnp.float32)
-            for half in range(2):
-                where = index * 2 + half
-                piece = part[:, half * span:(half + 1) * span]
-                if p == 0:
-                    acc[where] = piece
-                else:
-                    acc[where] += piece
-            return carry
-
-        lax.fori_loop(0, nz * caps // 2, multiply, 0)
+    rows_send = (rows + GROUP - 1) // GROUP * GROUP
 
     def x_copy(db, block, origin):
         target = (band + db) % nb
@@ -156,18 +169,43 @@
             send_sem=x_send.at[db, block], recv_sem=x_recv.at[db, block],
             device_id=(cell, target), device_id_type=MESH)
 
-    rows_send = (rows + GROUP - 1) // GROUP * GROUP
-    for db in range(1, nb):
-        for block in range(nq):
-            x_copy(db, block, band).start()
-    for db in range(1, nb):
-        for block in range(nq):
+    def multiply(p, begin, count):
+        blocks = opbuf[:, :, pl.ds(p * step, step)].reshape(nq * rows_pad, step)
+
+        def body(index, carry):
+            first = begin + index * 2
+            at = pl.multiple_of(first * span, 2 * span)
+            part = lax.dot_general(blocks, rolled[pl.ds(at, 2 * span), pl.ds(p * step, step)],
+                                   (((1,), (1,)), ((), ())), preferred_element_type=jnp.float32)
+            for half in range(2):
+                piece = part[:, half * span:(half + 1) * span]
+                if p == 0:
+                    acc[first + half] = piece
+                else:
+                    acc[first + half] += piece
+            return carry
+
+        lax.fori_loop(0, count // 2, body, 0)
+
+    for p in range(chunks):
+        forward[p].wait_recv()
+        if p < chunks - 1:
+            multiply(p, 0, nz * caps)
+        else:
+            for db in range(1, nb + 1):
+                multiply(p, (band + db) % nb * keep, keep)
+                if db < nb:
+                    for block in range(nq):
+                        x_copy(db, block, band).start()
+
+    def await_block(block):
+        for db in range(1, nb):
             x_copy(db, block, (band + nb - db) % nb).wait_recv()
 
-    def total(i, block):
-        value = acc[band * keep + i, block * rows_pad:block * rows_pad + rows_send, :]
+    def total(block):
+        value = acc[pl.ds(band * keep, keep), block * rows_pad:block * rows_pad + rows_send, :]
         for db in range(1, nb):
-            value = value + xbuf[(band + nb - db) % nb, i, block * rows_pad:block * rows_pad + rows_send, :]
+            value = value + xbuf[(band + nb - db) % nb, :, block * rows_pad:block * rows_pad + rows_send, :]
         return value
 
     def x0_copy(dz):
@@ -175,12 +213,16 @@
             src_ref=x0buf, dst_ref=x0buf, send_sem=x0_send.at[dz], recv_sem=x0_recv.at[0],
             device_id=(cell_of(dz, q), band), device_id_type=MESH)
 
+    await_block(0)
+
     @pl.when(z == 0)
     def _():
-        for i in range(keep):
-            x0buf[i] = total(i, 0)[0:GROUP]
+        x0buf[...] = total(0)[:, 0:GROUP, :]
         for dz in range(1, nz):
             x0_copy(dz).start()
+
+    for block in range(1, nq):
+        await_block(block)
 
     @pl.when(z != 0)
     def _():
@@ -195,26 +237,32 @@
             recv_sem=fin_recv.at[origin_cap, origin_z],
             device_id=(cell_of((band * keep + i) % nz, q), x), device_id_type=MESH)
 
+    def turn(value, amount):
+        return pltpu.roll(value, amount % span, 1)
+
     def three(value):
         value = jnp.where(lane < 3, value, 0.0)
-        value = value + pltpu.roll(value, 1, 1) + pltpu.roll(value, 2, 1)
+        value = value + turn(value, 1) + turn(value, 2)
         value = jnp.where(lane == 2, value, 0.0)
-        return value + pltpu.roll(value, span - 1, 1) + pltpu.roll(value, span - 2, 1)
+        return value + turn(value, -1) + turn(value, -2)
+
+    velocities = jnp.zeros((keep, GROUP, span), jnp.float32)
+    pole = x0buf[:, 0:1, :]
+    for block in range(nq):
+        value = total(block)
+        spread = (pole - value).reshape(keep * rows_send, span)
+        force = turn(value.reshape(keep * rows_send, span), -3)
+        dist_sq = three(spread * spread)
+        along = three(spread * force)
+        inverse = lax.rsqrt(dist_sq + blob_sq)
+        term = ((dist_sq + 2.0 * blob_sq) * force + along * spread) * (inverse * inverse * inverse)
+        term = jnp.where(lane < 3, term, 0.0).reshape(keep, rows_send, span)
+        term = term * weight_ref[z * nq + block, 0:rows_send, :]
+        for k in range(rows_send // GROUP):
+            velocities = velocities + term[:, k * GROUP:(k + 1) * GROUP]
 
     for i in range(keep):
-        velocity = jnp.zeros((GROUP, span), jnp.float32)
-        for block in range(nq):
-            value = total(i, block)
-            spread = x0buf[i, 0:1] - value
-            force = pltpu.roll(value, span - 3, 1)
-            dist_sq = three(spread * spread)
-            along = three(spread * force)
-            inverse = lax.rsqrt(dist_sq + blob_sq)
-            share = weight_ref[block * rows_pad:block * rows_pad + rows_send, :] * (inverse * inverse * inverse)
-            term = ((dist_sq + 2.0 * blob_sq) * force + along * spread) * share
-            term = jnp.where(lane < 3, term, 0.0)
-            for k in range(rows_send // GROUP):
-                velocity = velocity + term[k * GROUP:(k + 1) * GROUP]
+        velocity = velocities[i]
         vbuf[i] = velocity
         g = band * keep + i
         for x in range(nb):
@@ -245,9 +293,20 @@
 
     for copy in to_across + to_side + forward:
         copy.wait_send()
-    for dz in order:
-        shift_copy(z, dz).wait_send()
-        src_copy(z, dz).wait_send()
+    for way in range(2):
+        @pl.when(inner[way])
+        def _():
+            for copy in line_copy(z, way, True):
+                copy.wait_send()
+    for d in range(1, nz):
+        for way in range(2):
+            origin = (z - d, z + d)[way]
+            there = (z >= d, z + d < nz)[way]
+
+            @pl.when(jnp.logical_and(there, inner[way]))
+            def _():
+                for copy in line_copy(origin, way, False):
+                    copy.wait_send()
     for db in range(1, nb):
         for block in range(nq):
             x_copy(db, block, band).wait_send()
@@ -290,16 +349,13 @@
     op = jnp.stack([first, second, low], axis=2).reshape(rows, depth)
     op = jnp.pad(op, ((0, rows_pad - rows), (0, 0)))
     source = jnp.concatenate([positions, densities], axis=1)
-    source = jnp.pad(source, ((0, 0), (0, GROUP - 2 * comps), (0, 0), (0, 0)))
-    source = jnp.transpose(source.reshape(caps, GROUP, pairs, 2, lon), (0, 2, 1, 3, 4))
+    source = jnp.transpose(source.reshape(caps, 2 * comps, pairs, 2, lon), (0, 2, 1, 3, 4))
     first, second = source[..., 0, :], source[..., 1, :]
     source = jnp.concatenate([first, second[..., LANES:], second[..., :LANES]], axis=-1)
-    source = source.reshape(caps * pairs * GROUP, 3 * LANES)
+    source = source.reshape(caps, pairs * 2 * comps, 3 * LANES)
     shifts = jnp.broadcast_to(target_shift.reshape(caps * targets, 1), (caps * targets, LANES))
-    z = lax.axis_index("cell") // nq
-    mine = lax.dynamic_slice(weights, (z * nq * rows,), (nq * rows,)).reshape(nq, rows)
-    mine = jnp.pad(mine, ((0, 0), (0, rows_pad - rows))).reshape(nq * rows_pad, 1)
-    mine = jnp.broadcast_to(mine, (nq * rows_pad, span))
+    mine = weights.reshape(cells, rows, 1)
+    mine = jnp.pad(mine, ((0, 0), (0, rows_pad - rows), (0, 0)))
     dims = (nz, nq, bands, caps, targets, pairs, rows, rows_pad, lon, chunks)
     dma = pltpu.SemaphoreType.DMA
     hbm = pl.BlockSpec(memory_space=pl.ANY)
@@ -313,13 +369,14 @@
             pltpu.VMEM((nz,) + source.shape, jnp.bfloat16),
             pltpu.VMEM((nz, caps * targets, LANES), jnp.int32),
             pltpu.VMEM((nq, rows_pad, depth), jnp.bfloat16),
+            pltpu.VMEM((caps * pairs * GROUP, 3 * LANES), jnp.bfloat16),
             pltpu.VMEM((nz * caps * span, depth), jnp.bfloat16),
             pltpu.VMEM((nz * caps, nq * rows_pad, span), jnp.float32),
             pltpu.VMEM((bands, keep, nq * rows_pad, span), jnp.float32),
             pltpu.VMEM((keep, GROUP, span), jnp.float32),
             pltpu.VMEM((keep, GROUP, span), jnp.float32),
             pltpu.VMEM((caps, nz, GROUP, span), jnp.float32),
-            dma((nz,)), dma((nz,)), dma((nz,)), dma((nz,)),
+            dma((4, nz)), dma((nz,)), dma((4, nz)), dma((nz,)),
             dma((3, chunks)), dma((3, chunks)), dma((3,)),
             dma((bands, nq)), dma((bands, nq)), dma((nz,)), dma((1,)),
             dma((keep, bands)), dma((caps, nz)),

time: 77.3 us -> 67.3 us (0.87)
  Pallas kernels: 67.2 us -> 57.2 us
    pallas_call x1, Pallas kernels: 67.2 us -> 57.2 us  [per_device(): pl.pallas_call(functools.partial(kernel, dims), out_shape=jax.ShapeDtypeS...]
    broadcast_in_dim x2 -> x0, local copies, waits for them, and re-layouts: 0.81 us -> none  [per_device(): mine = jnp.broadcast_to(mine, (nq * rows_pad, span))]
where the time goes in v2:
time: 67.3 us; the launch traced here: 67 us
  Pallas kernels  57.2 us (85%)
  local copies, waits for them, and re-layouts  6.83 us (10%)
  other arithmetic  2.86 us (4%)
    pallas_call x1, Pallas kernels, per_device(): pl.pallas_call(functools.partial(kernel, dims), out_shape=jax.ShapeDtypeS...  57.2 us

profile of v2, /device:TPU:0, one launch (start us, length us, event | category | flops | bytes accessed | tf_op | source)
XLA Modules:
  0.0 67.0 jit_solution(1851392811117170898)
XLA Ops:
  0.0 1.0 %pad_maximum_fusion.1 = bf16[2,6,48,192]{3,2,1,0:T(8,128)(2,1)S(1)} fusion(bf16[2,3,48,192]{3,2,1,0:T(8,128)(2,1)} %param.6, bf16[2,3,48,192]{3,2,1,0:T(8,128)(2,1)} %param.5), kind=kLoop, calls=%fused_computation.1 | loop fusion | flops 110592 | bytes 442368 | tf_op jit(solution)/shard_map/concatenate | solution.py:351
  1.0 0.2 reshape.22
  1.2 0.3 copy.17
  1.5 0.2 fusion
  1.7 0.1 slice.37
  1.8 0.1 slice.38
  1.9 0.0 slice-start
  1.9 0.8 %pad_maximum_fusion.2.src_ref = bf16[2,144,384]{2,1,0:T(8,128)(2,1)} fusion(bf16[2,144,128]{2,1,0:T(8,128)(2,1)S(1)} %copy.12, bf16[2,144,64]{2,1,0:T(8,128)(2,1)S(1)} %copy.11, bf16[2,144,192]{2,1,0:T(8,128)(2,1)S(1)} %copy.10), kind=kLoop, calls=%fused_computation.3 | loop fusion | flops 663552 | bytes 442368 | tf_op jit(solution)/shard_map/concatenate | solution.py:354
  2.7 0.2 slice-done
  2.9 0.0 slice-start.1
  2.9 0.3 stack_reshape.4
  3.2 0.7 %slice-done.1 = bf16[40,48,128]{2,1,0:T(8,128)(2,1)S(1)} async-done(((bf16[40,48,192]{2,1,0:T(8,128)(2,1)}), bf16[40,48,128]{2,1,0:T(8,128)(2,1)S(1)}, s32[]{:S(2)}) %slice-start.1) | async-done | bytes 491544 | tf_op jit(solution)/shard_map/slice | solution.py:344
  3.9 1.0 %pad_maximum_fusion = bf16[40,24,3,128]{3,2,1,0:T(4,128)(2,1)S(1)} fusion(bf16[40,24,1,128]{3,2,1,0:T(2,128)(2,1)S(1)} %stack_reshape.4, bf16[40,24,2,128]{3,2,1,0:T(2,128)(2,1)S(1)} %bitcast.13), kind=kLoop, calls=%fused_computation | loop fusion | flops 1474560 | bytes 1474560 | tf_op jit(solution)/shard_map/stack | solution.py:349
  4.9 0.7 reshape.24
  5.6 0.0 copy-start
  5.6 0.0 copy-start.1
  5.6 1.0 %pad.8.op_ref = bf16[48,9216]{1,0:T(8,128)(2,1)} pad(bf16[40,9216]{1,0:T(8,128)(2,1)S(1)} %reshape.24, bf16[]{:T(256)} %constant.3.clone.1), padding=0_8x0_0 | pad | bytes 1622018 | tf_op jit(solution)/shard_map/jit(_pad)/pad | solution.py:350
  6.6 0.0 copy-done
  6.6 0.2 reshape.27
  6.9 0.8 %pad.9.weight_ref = f32[16,48,1]{2,1,0:T(8,128)} pad(f32[16,40,1]{2,1,0:T(8,128)S(1)} %reshape.27, f32[]{:T(128)} %constant.4.clone.1), padding=0_0x0_8x0_0 | pad | bytes 5636 | tf_op jit(solution)/shard_map/jit(_pad)/pad | solution.py:358
  7.6 0.0 copy-done.1
  7.6 0.1 broadcast_in_dim.7
  7.7 0.7 %broadcast_in_dim.8.shift_ref = s32[32,128]{1,0:T(8,128)} broadcast(s32[32]{0:T(128)S(1)} %broadcast_in_dim.7), dimensions={0} | broadcast | bytes 16512 | tf_op jit(solution)/shard_map/broadcast_in_dim | solution.py:356
  8.4 57.2 %shard_map.55 = f32[8,128]{1,0:T(8,128)} custom-call(bf16[2,144,384]{2,1,0:T(8,128)(2,1)} %pad_maximum_fusion.2.src_ref, s32[32,128]{1,0:T(8,128)} %broadcast_in_dim.8.shift_ref, bf16[48,9216]{1,0:T(8,128)(2,1)} %pad.8.op_ref, f32[16,48,1]{2,1,0:T(8,128)} %pad.9.weight_ref), custom_call_target="tpu_custom_call" | custom-call | tf_op jit(solution)/shard_map/pallas_call | solution.py:363
  65.5 0.7 %slice.33 = f32[2,128]{1,0:T(2,128)S(1)} slice(f32[8,128]{1,0:T(8,128)} %shard_map.55), slice={[0:2], [0:128]} | slice | bytes 2048 | tf_op jit(solution)/shard_map/slice | solution.py:388
  66.2 0.1 reshape.26
  66.3 0.7 copy.15
  (4 shorter events, 0.0 us)
Async XLA Ops:
  1.9 1.0 %slice-start = ((bf16[40,48,192]{2,1,0:T(8,128)(2,1)}), bf16[40,48,64]{2,1,0:T(8,128)(2,1)S(1)}, s32[]{:S(2)}) async-start(bf16[40,48,192]{2,1,0:T(8,128)(2,1)} %param.7), calls=%async_computation | async-start | bytes 983040 | tf_op jit(solution)/shard_map/slice | solution.py:345
  2.9 1.0 %slice-start.1 = ((bf16[40,48,192]{2,1,0:T(8,128)(2,1)}), bf16[40,48,128]{2,1,0:T(8,128)(2,1)S(1)}, s32[]{:S(2)}) async-start(bf16[40,48,192]{2,1,0:T(8,128)(2,1)} %param.7), calls=%async_computation.1 | async-start | bytes 983040 | tf_op jit(solution)/shard_map/slice | solution.py:344
  5.6 1.0 %copy-start = (f32[640]{0:T(1024)S(1)}, f32[640]{0:T(1024)}, u32[]{:S(2)}) copy-start(f32[640]{0:T(1024)} %param.9) | copy-start | bytes 7684
  5.6 2.0 %copy-start.1 = (s32[2,16]{1,0:T(2,128)S(1)}, s32[2,16]{1,0:T(2,128)}, u32[]{:S(2)}) copy-start(s32[2,16]{1,0:T(2,128)} %param.8) | copy-start | bytes 388

commit v3 on v2

--- a/solution.py
+++ b/solution.py
@@ -119,7 +119,10 @@
                     rolled[pl.ds(row, 2 * GROUP), pl.ds((p * 3 + tile) * LANES, LANES)] = both.astype(jnp.bfloat16)
             return carry
 
-        lax.fori_loop(0, caps * targets // 2, body, 0)
+        def twice(index, carry):
+            return body(index * 2 + 1, body(index * 2, carry))
+
+        lax.fori_loop(0, caps * targets // 4, twice, 0)
 
     own[0].wait()
     own[1].wait()
@@ -185,7 +188,10 @@
                     acc[first + half] += piece
             return carry
 
-        lax.fori_loop(0, count // 2, body, 0)
+        def twice(index, carry):
+            return body(index * 2 + 1, body(index * 2, carry))
+
+        lax.fori_loop(0, count // 4, twice, 0)
 
     for p in range(chunks):
         forward[p].wait_recv()

time: 67.3 us -> 61.7 us (0.917)
  Pallas kernels: 57.2 us -> 51.6 us
    pallas_call x1, Pallas kernels: 57.2 us -> 51.6 us  [per_device(): pl.pallas_call(functools.partial(kernel, dims), out_shape=jax.ShapeDtypeS...]
where the time goes in v3:
time: 61.7 us; the launch traced here: 61.4 us
  Pallas kernels  51.6 us (84%)
  local copies, waits for them, and re-layouts  6.83 us (11%)
  other arithmetic  2.86 us (5%)
    pallas_call x1, Pallas kernels, per_device(): pl.pallas_call(functools.partial(kernel, dims), out_shape=jax.ShapeDtypeS...  51.6 us

profile of v3, /device:TPU:0, one launch (start us, length us, event | category | flops | bytes accessed | tf_op | source)
XLA Modules:
  0.0 61.4 jit_solution(18041549742645488587)
XLA Ops:
  0.0 1.0 %pad_maximum_fusion.1 = bf16[2,6,48,192]{3,2,1,0:T(8,128)(2,1)S(1)} fusion(bf16[2,3,48,192]{3,2,1,0:T(8,128)(2,1)} %param.6, bf16[2,3,48,192]{3,2,1,0:T(8,128)(2,1)} %param.5), kind=kLoop, calls=%fused_computation.1 | loop fusion | flops 110592 | bytes 442368 | tf_op jit(solution)/shard_map/concatenate | solution.py:357
  1.0 0.2 reshape.22
  1.2 0.3 copy.17
  1.5 0.2 fusion
  1.7 0.1 slice.37
  1.8 0.1 slice.38
  1.9 0.0 slice-start
  1.9 0.8 %pad_maximum_fusion.2.src_ref = bf16[2,144,384]{2,1,0:T(8,128)(2,1)} fusion(bf16[2,144,128]{2,1,0:T(8,128)(2,1)S(1)} %copy.12, bf16[2,144,64]{2,1,0:T(8,128)(2,1)S(1)} %copy.11, bf16[2,144,192]{2,1,0:T(8,128)(2,1)S(1)} %copy.10), kind=kLoop, calls=%fused_computation.3 | loop fusion | flops 663552 | bytes 442368 | tf_op jit(solution)/shard_map/concatenate | solution.py:360
  2.7 0.2 slice-done
  2.9 0.0 slice-start.1
  2.9 0.3 stack_reshape.4
  3.2 0.7 %slice-done.1 = bf16[40,48,128]{2,1,0:T(8,128)(2,1)S(1)} async-done(((bf16[40,48,192]{2,1,0:T(8,128)(2,1)}), bf16[40,48,128]{2,1,0:T(8,128)(2,1)S(1)}, s32[]{:S(2)}) %slice-start.1) | async-done | bytes 491544 | tf_op jit(solution)/shard_map/slice | solution.py:350
  3.9 1.0 %pad_maximum_fusion = bf16[40,24,3,128]{3,2,1,0:T(4,128)(2,1)S(1)} fusion(bf16[40,24,1,128]{3,2,1,0:T(2,128)(2,1)S(1)} %stack_reshape.4, bf16[40,24,2,128]{3,2,1,0:T(2,128)(2,1)S(1)} %bitcast.13), kind=kLoop, calls=%fused_computation | loop fusion | flops 1474560 | bytes 1474560 | tf_op jit(solution)/shard_map/stack | solution.py:355
  4.9 0.7 %reshape.24 = bf16[40,9216]{1,0:T(8,128)(2,1)S(1)} reshape(bf16[40,24,3,128]{3,2,1,0:T(4,128)(2,1)S(1)} %pad_maximum_fusion) | data formatting | bytes 1474560 | tf_op jit(solution)/shard_map/reshape | solution.py:355
  5.6 0.0 copy-start
  5.6 0.0 copy-start.1
  5.6 1.0 %pad.8.op_ref = bf16[48,9216]{1,0:T(8,128)(2,1)} pad(bf16[40,9216]{1,0:T(8,128)(2,1)S(1)} %reshape.24, bf16[]{:T(256)} %constant.3.clone.1), padding=0_8x0_0 | pad | bytes 1622018 | tf_op jit(solution)/shard_map/jit(_pad)/pad | solution.py:356
  6.6 0.0 copy-done
  6.6 0.2 reshape.27
  6.9 0.8 %pad.9.weight_ref = f32[16,48,1]{2,1,0:T(8,128)} pad(f32[16,40,1]{2,1,0:T(8,128)S(1)} %reshape.27, f32[]{:T(128)} %constant.4.clone.1), padding=0_0x0_8x0_0 | pad | bytes 5636 | tf_op jit(solution)/shard_map/jit(_pad)/pad | solution.py:364
  7.6 0.0 copy-done.1
  7.6 0.1 broadcast_in_dim.7
  7.7 0.7 %broadcast_in_dim.8.shift_ref = s32[32,128]{1,0:T(8,128)} broadcast(s32[32]{0:T(128)S(1)} %broadcast_in_dim.7), dimensions={0} | broadcast | bytes 16512 | tf_op jit(solution)/shard_map/broadcast_in_dim | solution.py:362
  8.4 51.6 %shard_map.55 = f32[8,128]{1,0:T(8,128)} custom-call(bf16[2,144,384]{2,1,0:T(8,128)(2,1)} %pad_maximum_fusion.2.src_ref, s32[32,128]{1,0:T(8,128)} %broadcast_in_dim.8.shift_ref, bf16[48,9216]{1,0:T(8,128)(2,1)} %pad.8.op_ref, f32[16,48,1]{2,1,0:T(8,128)} %pad.9.weight_ref), custom_call_target="tpu_custom_call" | custom-call | tf_op jit(solution)/shard_map/pallas_call | solution.py:369
  60.0 0.7 %slice.33 = f32[2,128]{1,0:T(2,128)S(1)} slice(f32[8,128]{1,0:T(8,128)} %shard_map.55), slice={[0:2], [0:128]} | slice | bytes 2048 | tf_op jit(solution)/shard_map/slice | solution.py:394
  60.7 0.1 reshape.26
  60.8 0.7 %copy.15 = f32[2,3,16]{2,0,1:T(2,128)} copy(f32[2,3,16]{1,2,0:T(8,128)S(1)} %slice_bitcast_fusion.1) | data formatting | bytes 768 | tf_op jit(solution)/shard_map/transpose | solution.py:395
  (4 shorter events, 0.0 us)
Async XLA Ops:
  1.9 1.0 %slice-start = ((bf16[40,48,192]{2,1,0:T(8,128)(2,1)}), bf16[40,48,64]{2,1,0:T(8,128)(2,1)S(1)}, s32[]{:S(2)}) async-start(bf16[40,48,192]{2,1,0:T(8,128)(2,1)} %param.7), calls=%async_computation | async-start | bytes 983040 | tf_op jit(solution)/shard_map/slice | solution.py:351
  2.9 1.0 %slice-start.1 = ((bf16[40,48,192]{2,1,0:T(8,128)(2,1)}), bf16[40,48,128]{2,1,0:T(8,128)(2,1)S(1)}, s32[]{:S(2)}) async-start(bf16[40,48,192]{2,1,0:T(8,128)(2,1)} %param.7), calls=%async_computation.1 | async-start | bytes 983040 | tf_op jit(solution)/shard_map/slice | solution.py:350
  5.6 1.0 %copy-start = (f32[640]{0:T(1024)S(1)}, f32[640]{0:T(1024)}, u32[]{:S(2)}) copy-start(f32[640]{0:T(1024)} %param.9) | copy-start | bytes 7684
  5.6 2.0 %copy-start.1 = (s32[2,16]{1,0:T(2,128)S(1)}, s32[2,16]{1,0:T(2,128)}, u32[]{:S(2)}) copy-start(s32[2,16]{1,0:T(2,128)} %param.8) | copy-start | bytes 388
